TPU v7x, 128 devices: a whole 4x4x4 slice. The times are simulated.
128 devices in a mesh: row: 8 (over z, y_hi), col: 16 (over x, y_lo, core).
Axes of the slice: x: 4, y: 4 (y_hi: 2, y_lo: 2; y = y_hi * 2 + y_lo), z: 4, core: 2. Of those that a mesh axis runs over, the one named last changes fastest.
Arguments:
- tokens_in: bfloat16 [16384, 1408], P(('row', 'col')), may hold values from -300 to 300
- ln1_gain: bfloat16 [1408], replicated, may hold values from 0.099609375 to 1.8984375
- ln1_bias: bfloat16 [1408], replicated, may hold values from -3 to 3
- qkv_weight: bfloat16 [1408, 4224], P('row', 'col'), may hold values from -0.8 to 0.8
- qkv_bias: bfloat16 [4224], P('col'), may hold values from -3 to 3
- proj_weight: bfloat16 [1408, 1408], P('col', 'row'), may hold values from -0.15625 to 0.15625
- proj_bias: bfloat16 [1408], replicated, may hold values from -3 to 3
- ln2_gain: bfloat16 [1408], replicated, may hold values from 0.099609375 to 1.8984375
- ln2_bias: bfloat16 [1408], replicated, may hold values from -3 to 3
- fc1_weight: bfloat16 [1408, 6144], P('row', 'col'), may hold values from -0.15625 to 0.15625
- fc1_bias: bfloat16 [6144], P('col'), may hold values from -3 to 3
- fc2_weight: bfloat16 [1408, 6144], P('row', 'col'), may hold values from -0.078125 to 0.078125
- fc2_bias: bfloat16 [1408], replicated, may hold values from -3 to 3
Outputs:
- tokens_out: bfloat16 [16384, 1408], P(('row', 'col'))
All inputs are finite; a program needn't handle non-finite values.
Results may differ from a plain program's by a relative error of at most 0.01.
Values may be sent and summed in bfloat16 or wider, within the bound.
A program may use at most 64 MiB of HBM per device.

v0:
```python
import jax
import jax.numpy as jnp
from jax import lax
from jax.sharding import PartitionSpec as P

HEADS = 16


def laid_out(pieces, dim):
    dims = list(pieces.shape[1:])
    dims[dim] *= pieces.shape[0]
    return jnp.moveaxis(pieces, 0, dim).reshape(dims)


def copy_for_each(value, axis):
    size = lax.axis_size(axis)
    return lax.all_to_all(
        jnp.broadcast_to(value[None], (size, *value.shape)), axis, 0, 0, tiled=True
    )


def collect(value, axis, dim):
    return laid_out(copy_for_each(value, axis), dim)


def norm_local(values, gain, bias):
    mean = jnp.mean(values, axis=-1, keepdims=True)
    centred = values - mean
    var = jnp.mean(centred * centred, axis=-1, keepdims=True)
    return centred * lax.rsqrt(var + 1e-06) * gain.astype(jnp.float32) + bias.astype(jnp.float32)


def attend(qkv, heads):
    length = qkv.shape[0]
    head_size = qkv.shape[1] // (3 * heads)
    parts = qkv.reshape(length, heads, 3, head_size)
    query = parts[:, :, 0]
    keys = parts[:, :, 1]
    values = parts[:, :, 2]
    block = min(512, length)
    blocks = query.reshape(length // block, block, heads, head_size)
    scale = 1.0 / head_size**0.5

    def one_block(qblock):
        scores = (
            jnp.einsum("qhe,khe->hqk", qblock, keys, preferred_element_type=jnp.float32) * scale
        )
        top = jnp.max(scores, axis=-1, keepdims=True)
        expo = jnp.exp(scores - top)
        probs = (expo / jnp.sum(expo, axis=-1, keepdims=True)).astype(jnp.bfloat16)
        mixed = jnp.einsum("hqk,khe->qhe", probs, values, preferred_element_type=jnp.float32)
        return mixed.astype(jnp.bfloat16).reshape(block, heads * head_size)

    return lax.map(one_block, blocks).reshape(length, heads * head_size)


def project_back(left, right):
    return lax.dot_general(
        left, right, (((1,), (1,)), ((), ())), preferred_element_type=jnp.float32
    )


def local(
    tokens_in,
    ln1_gain,
    ln1_bias,
    qkv_weight,
    qkv_bias,
    proj_weight,
    proj_bias,
    ln2_gain,
    ln2_bias,
    fc1_weight,
    fc1_bias,
    fc2_weight,
    fc2_bias,
):
    local_heads = HEADS // lax.axis_size("col")
    own_rows = tokens_in.shape[0]
    inputs = tokens_in.astype(jnp.float32)
    qkv_full = collect(qkv_weight, "row", 0)
    proj_full = collect(proj_weight, "row", 1)
    fc1_full = collect(fc1_weight, "row", 0)
    fc2_full = collect(fc2_weight, "row", 0)
    qkv_shift = qkv_bias.astype(jnp.float32)
    fc1_shift = fc1_bias.astype(jnp.float32)
    ln1 = norm_local(inputs, ln1_gain, ln1_bias).astype(jnp.bfloat16)
    product = (
        jnp.dot(
            lax.all_gather(ln1, "col", axis=0, tiled=True),
            qkv_full,
            preferred_element_type=jnp.float32,
        )
        + qkv_shift
    )
    qkv = product.astype(jnp.bfloat16)
    attn = attend(qkv, local_heads)
    proj_whole = lax.all_gather(proj_full, "col", axis=0, tiled=True)
    groups = lax.axis_size("col")
    width = proj_whole.shape[0] // groups
    own_heads = lax.all_to_all(attn, "col", split_axis=0, concat_axis=1, tiled=True)
    lefts = own_heads.reshape(own_rows, groups, width)
    rights = proj_whole.reshape(groups, width, proj_whole.shape[1])
    group_parts = jnp.einsum("rgc,gcd->grd", lefts, rights, preferred_element_type=jnp.float32)
    group_parts = lax.optimization_barrier(group_parts.astype(jnp.bfloat16))
    attn_sum = jnp.sum(group_parts.astype(jnp.float32), axis=0)
    resid = inputs + attn_sum + proj_bias.astype(jnp.float32)
    ln2 = norm_local(resid, ln2_gain, ln2_bias).astype(jnp.bfloat16)
    product = (
        jnp.dot(
            lax.all_gather(ln2, "col", axis=0, tiled=True),
            fc1_full,
            preferred_element_type=jnp.float32,
        )
        + fc1_shift
    )
    hidden = jax.nn.gelu(product, approximate=False).astype(jnp.bfloat16)
    mlp_sum = lax.psum_scatter(
        project_back(hidden, fc2_full).astype(jnp.bfloat16), "col", scatter_dimension=0, tiled=True
    ).astype(jnp.float32)
    result = resid + mlp_sum + fc2_bias.astype(jnp.float32)
    return result.astype(jnp.bfloat16)


def solution(mesh):
    in_specs = (
        P(("row", "col"), None),
        P(),
        P(),
        P("row", "col"),
        P("col"),
        P("col", "row"),
        P(),
        P(),
        P(),
        P("row", "col"),
        P("col"),
        P("row", "col"),
        P(),
    )
    out_specs = P(("row", "col"), None)
    return jax.shard_map(local, mesh=mesh, in_specs=in_specs, out_specs=out_specs, check_vma=False)
```

profile of v0, /device:TPU:1, one launch (start us, length us, event | category | flops | bytes accessed | tf_op | source)
XLA Modules:
  0.0 273.0 jit_solution(1702944770370740477)
XLA Ops:
  6.5 1.1 convert_reduce_fusion.1
  7.7 1.2 fusion.25
  10.3 2.0 fusion.28
  13.1 17.3 %all_to_all.36 = bf16[8,88,176]{2,1,0:T(8,128)(2,1)S(1)} all-to-all(bf16[8,88,176]{2,1,0:T(8,128)(2,1)S(1)} %broadcast_in_dim.15), channel_id=1, replica_groups=mesh['row'=8,'col'=16] {'row'}, dimensions={0} | all-to-all | bytes 495616 | tf_op jit(solution)/shard_map/all_to_all | solution.py:17
  30.4 2.0 broadcast_in_dim.14
  32.4 3.6 %all-to-all-start = ((bf16[8,176,264]{2,1,0:T(8,128)(2,1)}), bf16[8,176,264]{2,1,0:T(8,128)(2,1)S(1)}, u32[]{:S(2)}, u32[]{:S(2)}) async-start(bf16[8,176,264]{2,1,0:T(8,128)(2,1)} %broadcast_in_dim.14), calls=%async_computation | async-start | bytes 2162688 | tf_op jit(solution)/shard_map/all_to_all | solution.py:17
  36.1 1.1 reshape.95
  37.2 27.2 %all-to-all-done = bf16[8,176,264]{2,1,0:T(8,128)(2,1)S(1)} async-done(((bf16[8,176,264]{2,1,0:T(8,128)(2,1)}), bf16[8,176,264]{2,1,0:T(8,128)(2,1)S(1)}, u32[]{:S(2)}, u32[]{:S(2)}) %all-to-all-start) | async-done | bytes 743456 | tf_op jit(solution)/shard_map/all_to_all | solution.py:17
  64.5 3.0 %all-gather.4.cloned.1.call-done = bf16[2048,1408]{1,0:T(8,128)(2,1)} async-done(((bf16[128,1408]{1,0:T(8,128)(2,1)}), bf16[2048,1408]{1,0:T(8,128)(2,1)}) %all-gather.4.cloned.1.call-update) | async-done | bytes 5767184 | tf_op jit(solution)/shard_map/all_gather | solution.py:90
  67.5 4.5 %fusion.22 = bf16[2048,264]{0,1:T(8,128)(2,1)S(1)} fusion(bf16[2048,1408]{1,0:T(8,128)(2,1)} %all-gather.4.cloned.1.call-done, bf16[1408,264]{1,0:T(8,128)(2,1)S(1)} %bitcast.58, f32[264]{0:T(512)S(1)} %convert_element_type.74), kind=kOutput, calls=%fused_computation.38 | convolution fusion | flops 1523613696 | bytes 7592992 | tf_op jit(solution)/shard_map/dot_general | solution.py:89
  72.5 11.3 %while.10 = (s32[]{:T(128)}, bf16[4,512,88]{1,2,0:T(8,128)(2,1)S(1)}, bf16[4,512,1,88]{1,3,2,0:T(8,128)(2,1)S(1)}, bf16[2048,1,88]{0,2,1:T(8,128)(2,1)S(1)}, bf16[2048,1,88]{0,2,1:T(8,128)(2,1)S(1)}, /*index=5*/s32[]{:T(128)}) while((s32[]{:T(128)}, bf16[4,512,88]{1,2,0:T(8,128)(2,1)S(1)}, bf16[4,512,1,88]{1,3,2,0:T(8,128)(2,1)S(1)}, ...), condition=%wide.region_5.6_spmd, body=%wide.region_2.5_spmd.sunk | while | flops 378579968 | bytes 13494349 | solution.py:54
  73.4 0.8 fusion.72
  74.2 1.1 fusion.73
  75.4 0.8 multiply_reduce_fusion.3
  76.2 0.8 fusion.72
  77.0 1.1 fusion.73
  78.2 0.8 multiply_reduce_fusion.3
  79.8 1.1 fusion.73
  81.0 0.8 multiply_reduce_fusion.3
  82.6 1.1 fusion.73
  84.1 0.8 copy.25
  85.0 5.6 %all-to-all-start.1 = ((bf16[16,128,88]{1,2,0:T(8,128)(2,1)}), bf16[16,128,88]{1,2,0:T(8,128)(2,1)S(1)}, u32[]{:S(2)}, u32[]{:S(2)}) async-start(bf16[16,128,88]{1,2,0:T(8,128)(2,1)} %copy.25), calls=%async_computation.1 | async-start | bytes 720896 | tf_op jit(solution)/shard_map/all_to_all | solution.py:101
  90.6 20.3 %all-gather.6.cloned.1.call-done = bf16[1408,1408]{1,0:T(8,128)(2,1)} async-done(((bf16[88,1408]{1,0:T(8,128)(2,1)}), bf16[1408,1408]{1,0:T(8,128)(2,1)}) %all-gather.6.cloned.1.call-update) | async-done | bytes 3964944 | tf_op jit(solution)/shard_map/all_gather | solution.py:98
  111.0 3.8 %convolution_convert_fusion.1 = bf16[16,128,1408]{2,1,0:T(8,128)(2,1)S(1)} fusion(bf16[16,88,1408]{2,1,0:T(8,128)(2,1)} %bitcast.56, bf16[16,128,88]{1,2,0:T(8,128)(2,1)S(1)} %all-to-all-done.1), kind=kOutput, calls=%fused_computation.17 | convolution fusion | flops 510394368 | bytes 10092544 | tf_op jit(solution)/shard_map/rgc,gcd->grd/dot_general | solution.py:104
  116.2 0.9 add_convert_fusion.1
  117.3 31.3 %all_to_all.37 = bf16[8,176,384]{2,1,0:T(8,128)(2,1)S(1)} all-to-all(bf16[8,176,384]{2,1,0:T(8,128)(2,1)S(1)} %broadcast_in_dim.16), channel_id=1, replica_groups=mesh['row'=8,'col'=16] {'row'}, dimensions={0} | all-to-all | bytes 2162688 | tf_op jit(solution)/shard_map/all_to_all | solution.py:17
  148.7 1.1 broadcast_in_dim.17
  149.8 3.6 %all-to-all-start.4 = ((bf16[8,176,384]{2,1,0:T(8,128)(2,1)}), bf16[8,176,384]{2,1,0:T(8,128)(2,1)S(1)}, u32[]{:S(2)}, u32[]{:S(2)}) async-start(bf16[8,176,384]{2,1,0:T(8,128)(2,1)} %broadcast_in_dim.17), calls=%async_computation.4 | async-start | bytes 2162688 | tf_op jit(solution)/shard_map/all_to_all | solution.py:17
  153.6 25.1 %all-to-all-done.4 = bf16[8,176,384]{2,1,0:T(8,128)(2,1)S(1)} async-done(((bf16[8,176,384]{2,1,0:T(8,128)(2,1)}), bf16[8,176,384]{2,1,0:T(8,128)(2,1)S(1)}, u32[]{:S(2)}, u32[]{:S(2)}) %all-to-all-start.4) | async-done | bytes 1081376 | tf_op jit(solution)/shard_map/all_to_all | solution.py:17
  178.8 16.4 %convolution_convert_fusion = bf16[2048,1408]{1,0:T(8,128)(2,1)} fusion(bf16[1408,384]{1,0:T(8,128)(2,1)S(1)} %bitcast.60, bf16[2048,1408]{1,0:T(8,128)(2,1)} %all-gather.8.cloned.1.call-done, bf16[1408,384]{1,0:T(8,128)(2,1)S(1)} %bitcast.59, f32[384]{0:T(512)S(1)} %convert_element_type.82), kind=kOutput, calls=%fused_computation.16 | convolution fusion | flops 4483973120 | bytes 13698560 | tf_op jit(solution)/shard_map/dot_general | solution.py:58
  195.9 68.7 %reduce-scatter.2.cloned.1.call-done = bf16[128,1408]{1,0:T(8,128)(2,1)} async-done(((bf16[2048,1408]{1,0:T(8,128)(2,1)}), bf16[128,1408]{1,0:T(8,128)(2,1)}) %reduce-scatter.2.cloned.1.call-update) | async-done | bytes 360464 | tf_op jit(solution)/shard_map/reduce_scatter | solution.py:118
  264.6 1.9 add_convert_fusion
  (55 shorter events, 8.1 us)
Async XLA Ops:
  6.5 61.0 %all-gather.4.cloned.1.call-start = ((), (), s32[]{:S(2)}) async-start(), calls=%async_computation.6 | async-start | bytes 6127616 | tf_op jit(solution)/shard_map/all_gather | solution.py:90
  12.3 24.9 %copy-start.7 = (bf16[264]{0:T(512)(128)(2,1)S(1)}, bf16[264]{0:T(512)(128)(2,1)}, u32[]{:S(2)}) copy-start(bf16[264]{0:T(512)(128)(2,1)} %param.19) | copy-start | bytes 1588
  32.4 32.1 %all-to-all-start = ((bf16[8,176,264]{2,1,0:T(8,128)(2,1)}), bf16[8,176,264]{2,1,0:T(8,128)(2,1)S(1)}, u32[]{:S(2)}, u32[]{:S(2)}) async-start(bf16[8,176,264]{2,1,0:T(8,128)(2,1)} %broadcast_in_dim.14), calls=%async_computation | async-start | bytes 2162688 | tf_op jit(solution)/shard_map/all_to_all | solution.py:17
  36.0 75.0 %all-gather.6.cloned.1.call-start = ((), (), s32[]{:S(2)}) async-start(), calls=%async_computation.7 | async-start | bytes 4212736 | tf_op jit(solution)/shard_map/all_gather | solution.py:98
  72.5 18.1 %copy-start.3 = (bf16[1408]{0:T(1024)(128)(2,1)S(1)}, bf16[1408]{0:T(1024)(128)(2,1)}, u32[]{:S(2)}) copy-start(bf16[1408]{0:T(1024)(128)(2,1)} %param.21) | copy-start | bytes 8452
  72.5 18.1 %copy-start.4 = (bf16[1408]{0:T(1024)(128)(2,1)S(1)}, bf16[1408]{0:T(1024)(128)(2,1)}, u32[]{:S(2)}) copy-start(bf16[1408]{0:T(1024)(128)(2,1)} %param.22) | copy-start | bytes 8452
  72.5 18.1 %copy-start.5 = (bf16[1408]{0:T(1024)(128)(2,1)S(1)}, bf16[1408]{0:T(1024)(128)(2,1)}, u32[]{:S(2)}) copy-start(bf16[1408]{0:T(1024)(128)(2,1)} %param.23) | copy-start | bytes 8452
  85.0 26.0 %all-to-all-start.1 = ((bf16[16,128,88]{1,2,0:T(8,128)(2,1)}), bf16[16,128,88]{1,2,0:T(8,128)(2,1)S(1)}, u32[]{:S(2)}, u32[]{:S(2)}) async-start(bf16[16,128,88]{1,2,0:T(8,128)(2,1)} %copy.25), calls=%async_computation.1 | async-start | bytes 720896 | tf_op jit(solution)/shard_map/all_to_all | solution.py:101
  90.5 88.2 %all-gather.8.cloned.1.call-start = ((), (), s32[]{:S(2)}) async-start(), calls=%async_computation.8 | async-start | bytes 6127616 | tf_op jit(solution)/shard_map/all_gather | solution.py:111
  114.8 1.0 copy-start
  115.8 1.4 copy-start.1
  116.0 32.7 %copy-start.2 = (bf16[176,384]{1,0:T(8,128)(2,1)S(1)}, bf16[176,384]{1,0:T(8,128)(2,1)}, u32[]{:S(2)}) copy-start(bf16[176,384]{1,0:T(8,128)(2,1)} %param.26) | copy-start | bytes 405508
  117.2 36.4 %copy-start.8 = (bf16[384]{0:T(512)(128)(2,1)S(1)}, bf16[384]{0:T(512)(128)(2,1)}, u32[]{:S(2)}) copy-start(bf16[384]{0:T(512)(128)(2,1)} %param.25) | copy-start | bytes 2308
  149.8 29.0 %all-to-all-start.4 = ((bf16[8,176,384]{2,1,0:T(8,128)(2,1)}), bf16[8,176,384]{2,1,0:T(8,128)(2,1)S(1)}, u32[]{:S(2)}, u32[]{:S(2)}) async-start(bf16[8,176,384]{2,1,0:T(8,128)(2,1)} %broadcast_in_dim.17), calls=%async_computation.4 | async-start | bytes 2162688 | tf_op jit(solution)/shard_map/all_to_all | solution.py:17
  153.4 111.2 %reduce-scatter.2.cloned.1.call-start = ((), (), s32[]{:S(2)}) async-start(), calls=%async_computation.9 | async-start | bytes 6127616 | tf_op jit(solution)/shard_map/reduce_scatter | solution.py:118
  195.2 0.7 copy-start.6
Sparse Core Ops, SparseCore 0:
  12.4 55.0 all-gather.3
  69.2 41.7 all-gather.5
  117.3 55.6 all-gather.7
  195.3 69.2 reduce-scatter.1
where the time goes:
time: 275 us; the launch traced here: 273 us
  waiting for transfers between devices  145 us (53%)
  blocking collectives  48.6 us (18%)
  matrix products  32.7 us (12%)
  between operations  13.4 us (5%)
  other arithmetic  13.1 us (5%)
  starting transfers between devices  13 us (5%)
  local copies, waits for them, and re-layouts  7.61 us (3%)
    reduce_scatter x1, waiting for transfers between devices, local(): lax.psum_scatter(project_back(hidden, fc2_full).astype(jnp.bfloat16), 'co...  68.7 us
    all_to_all x2, waiting for transfers between devices, copy_for_each(): lax.all_to_all(jnp.broadcast_to(value[None], (size, *value.shape)), axis,...  52.4 us
    all_to_all x2, blocking collectives, copy_for_each(): lax.all_to_all(jnp.broadcast_to(value[None], (size, *value.shape)), axis,...  48.6 us
    all_gather x1, waiting for transfers between devices, local(): proj_whole = lax.all_gather(proj_full, 'col', axis=0, tiled=True)  20.3 us
    dot_general x1, matrix products, project_back(): lax.dot_general(left, right, (((1,), (1,)), ((), ())), preferred_element_...  16.4 us
    all_to_all x2, starting transfers between devices, copy_for_each(): lax.all_to_all(jnp.broadcast_to(value[None], (size, *value.shape)), axis,...  7.15 us
    all_to_all x1, starting transfers between devices, local(): lax.all_to_all(attn, 'col', split_axis=0, concat_axis=1, tiled=True)  5.57 us
  transfers between devices with their start and end apart: 7, of which 5 were waited for; matrix products, arithmetic and copies ran while one was open for 8% of the time, Pallas kernels for 0%

commit v1 on v0

v1 whole, which is shorter than its diff:
```python
import jax
import jax.numpy as jnp
from jax import lax
from jax.experimental import pallas as pl
from jax.experimental.pallas import tpu as pltpu
from jax.sharding import PartitionSpec as P

MESH = pl.DeviceIdType.MESH
F32 = jnp.float32
BF16 = jnp.bfloat16
D = 1408
HEAD = 88
COPIES = 96
SCALE = (1.0 / HEAD**0.5) * 1.4426950408889634
NT = (((1,), (1,)), ((), ()))


def norm(values, gain, bias):
    mean = jnp.mean(values, axis=-1, keepdims=True)
    centred = values - mean
    var = jnp.mean(centred * centred, axis=-1, keepdims=True)
    return centred * lax.rsqrt(var + 1e-06) * gain + bias


def kernel(
    tok, prm, wq, wp, f1, f2, out,
    X, WQ, WP, F1, F2, FB, QKV, O, OA, RES, H, PART, SS, SD, KEEP, D2S, PS, MS, RA, RB, RL, RR,
    send, recv, asend, arecv, lsem,
):
    r = lax.axis_index("row")
    c = lax.axis_index("col")
    z, yh = r // 2, r % 2
    x, yl, core = c // 4, (c // 2) % 2, c % 2
    y = yh * 2 + yl
    chip = c // 2

    def plus(v, n):
        return lax.rem(v + n, 4)

    def at_x(v):
        return (r, v * 4 + yl * 2 + core)

    def at_y(v):
        return (z * 2 + v // 2, x * 4 + lax.rem(v, 2) * 2 + core)

    def at_z(v):
        return (v * 2 + yh, c)

    xp, xm = at_x(plus(x, 1)), at_x(plus(x, 3))
    yp, ym = at_y(plus(y, 1)), at_y(plus(y, 3))
    zp, zm = at_z(plus(z, 1)), at_z(plus(z, 3))
    ylp = (r, x * 4 + (1 - yl) * 2 + core)
    yh2 = (z * 2 + 1 - yh, c)
    dd = (r, x * 4 + yl * 2 + 1 - core)

    barrier = pltpu.get_barrier_semaphore()
    for peer in (yp, ym, zp, zm, yh2):
        pl.semaphore_signal(barrier, inc=1, device_id=peer, device_id_type=MESH)

    def greet(i, carry):
        pl.semaphore_signal(
            barrier, inc=1, device_id=(r, lax.rem(c + i, 16)), device_id_type=MESH
        )
        return carry

    lax.fori_loop(1, 16, greet, 0)

    def cols(v):
        return pl.ds(pl.multiple_of(v * 384, 384), 384)

    def lanes(xv, ylv, cv):
        return pl.ds(pl.multiple_of(cv * 1024 + xv * 256 + ylv * 128, 128), 128)

    def wide(xv):
        return pl.ds(pl.multiple_of(core * 1024 + xv * 256, 256), 256)

    loads = [
        pltpu.make_async_copy(wq, WQ.at[z, yh], lsem.at[0]),
        pltpu.make_async_copy(f1, F1.at[z, yh, :, cols(yl)], lsem.at[1]),
        pltpu.make_async_copy(f2, F2.at[z, yh, :, cols(yl)], lsem.at[2]),
        pltpu.make_async_copy(wp, WP.at[z, yh, :, lanes(x, yl, core)], lsem.at[3]),
    ]
    for load in loads:
        load.start()

    started = []

    def go(src, dst, dev):
        i = len(started)
        copy = pltpu.make_async_remote_copy(
            src_ref=src, dst_ref=dst, send_sem=send.at[i], recv_sem=recv.at[i],
            device_id=dev, device_id_type=MESH,
        )
        copy.start()
        started.append(copy)
        return copy

    def push(ref, dev):
        return go(ref, ref, dev)

    inputs = tok[...].astype(F32)
    X[chip, core] = norm(inputs, prm[0:1, :], prm[1:2, :]).astype(BF16)
    FB[yl] = jnp.broadcast_to(prm[6:7, 384:768], (8, 384))
    for load in loads:
        load.wait()
    pl.semaphore_wait(barrier, 20)

    own = X.at[chip, core]
    wq_own = WQ.at[z, yh]
    q_y2 = push(wq_own, yh2)
    q_p = push(wq_own, zp)
    q_m = push(wq_own, zm)
    a_p = push(own, xp)
    a_m = push(own, xm)
    a_y = push(own, ylp)
    a_d = push(own, dd)
    b_y = push(FB.at[yl], ylp)

    def f_piece(F, zv, yv):
        return F.at[zv, yv // 2, :, cols(lax.rem(yv, 2))]

    def f_half(F, zv, yv, first):
        rows = pl.ds(0, 96) if first else pl.ds(96, 80)
        return F.at[zv, yv // 2, rows, cols(lax.rem(yv, 2))]

    def p_half(yv, first):
        rows = pl.ds(0, 96) if first else pl.ds(96, 80)
        return WP.at[z, yv // 2, rows, lanes(x, lax.rem(yv, 2), core)]

    p_own = WP.at[z, yh, :, lanes(x, yl, core)]
    py_p = push(p_own, yp)
    py_m = push(p_own, ym)
    f2z_p = push(f_piece(F2, z, y), zp)
    f2z_m = push(f_piece(F2, z, y), zm)
    f1y_p = push(f_piece(F1, z, y), yp)
    f1y_m = push(f_piece(F1, z, y), ym)

    q_y2.wait_recv()
    wq_other = WQ.at[z, 1 - yh]
    q2_p = push(wq_other, zp)
    q2_m = push(wq_other, zm)
    q_p.wait_recv()
    q_pf = push(WQ.at[plus(z, 3), yh, pl.ds(0, 96)], zp)
    q_m.wait_recv()
    q_mf = push(WQ.at[plus(z, 1), yh, pl.ds(96, 80)], zm)

    def chip_of(xv, ylv):
        return xv * 2 + ylv

    left, right, far = plus(x, 3), plus(x, 1), plus(x, 2)
    a_p.wait_recv()
    l1 = X.at[chip_of(left, yl), core]
    a_pf = push(X.at[chip_of(left, yl), core, pl.ds(0, 64)], xp)
    l1_d = push(l1, dd)
    a_m.wait_recv()
    r1 = X.at[chip_of(right, yl), core]
    a_mf = push(X.at[chip_of(right, yl), core, pl.ds(64, 64)], xm)
    r1_d = push(r1, dd)
    a_y.wait_recv()
    p0 = X.at[chip_of(x, 1 - yl), core]
    y_p = push(p0, xp)
    y_m = push(p0, xm)
    p0_d = push(p0, dd)

    q2_p.wait_recv()
    q2_pf = push(WQ.at[plus(z, 3), 1 - yh, pl.ds(0, 96)], zp)
    q2_m.wait_recv()
    q2_mf = push(WQ.at[plus(z, 1), 1 - yh, pl.ds(96, 80)], zm)

    def qkv(where):
        block = X[where].reshape(256, D)
        product = jnp.dot(block, WQ[...].reshape(D, 384), preferred_element_type=F32)
        QKV[where] = (product + prm[6:7, 0:384]).astype(BF16)

    a_pf.wait_recv()
    a_mf.wait_recv()
    d2 = X.at[chip_of(far, yl), core]
    d2_y = push(d2, ylp)
    d2_d = push(d2, dd)

    py_p.wait_recv()
    py_pf = push(p_half(plus(y, 3), True), yp)
    py_m.wait_recv()
    py_mf = push(p_half(plus(y, 1), False), ym)
    f2z_p.wait_recv()
    f2z_pf = push(f_half(F2, plus(z, 3), y, True), zp)
    f2z_m.wait_recv()
    f2z_mf = push(f_half(F2, plus(z, 1), y, False), zm)
    f1y_p.wait_recv()
    f1y_pf = push(f_half(F1, z, plus(y, 3), True), yp)
    f1y_m.wait_recv()
    f1y_mf = push(f_half(F1, z, plus(y, 1), False), ym)

    for copy in (q_pf, q_mf, q2_pf, q2_mf, a_d):
        copy.wait_recv()
    qkv(chip)
    l1_d.wait_recv()
    qkv(chip_of(left, yl))
    r1_d.wait_recv()
    qkv(chip_of(right, yl))
    p0_d.wait_recv()
    qkv(chip_of(x, 1 - yl))

    py_pf.wait_recv()
    py_mf.wait_recv()
    p_zown = WP.at[z, :, :, wide(x)]
    pz_p = push(p_zown, zp)
    pz_m = push(p_zown, zm)

    d2_d.wait_recv()
    qkv(chip_of(far, yl))

    y_p.wait_recv()
    pl1 = X.at[chip_of(left, 1 - yl), core]
    pl1_d = push(pl1, dd)
    y_m.wait_recv()
    pr1 = X.at[chip_of(right, 1 - yl), core]
    pr1_d = push(pr1, dd)
    d2_y.wait_recv()
    pd2 = X.at[chip_of(far, 1 - yl), core]
    pd2_d = push(pd2, dd)

    f2z_pf.wait_recv()
    f2z_mf.wait_recv()
    f2_yown = F2.at[:, yh, :, cols(yl)]
    f2y_p = push(f2_yown, yp)
    f2y_m = push(f2_yown, ym)
    f1y_pf.wait_recv()
    f1y_mf.wait_recv()
    f1_zown = F1.at[z]
    f1z_p = push(f1_zown, zp)
    f1z_m = push(f1_zown, zm)
    pz_p.wait_recv()
    pz_pf = push(WP.at[plus(z, 3), 0, :, wide(x)], zp)
    pz_m.wait_recv()
    pz_mf = push(WP.at[plus(z, 1), 1, :, wide(x)], zm)

    pl1_d.wait_recv()
    qkv(chip_of(left, 1 - yl))
    pr1_d.wait_recv()
    qkv(chip_of(right, 1 - yl))
    pd2_d.wait_recv()
    qkv(chip_of(far, 1 - yl))

    def attend(tc):
        q = QKV[tc, :, 0:128]
        k = QKV[:, :, 128:256].reshape(2048, 128)
        v = QKV[:, :, 256:384].reshape(2048, 128)
        s = lax.dot_general(q, k, NT, preferred_element_type=F32)
        top = jnp.max(s, axis=-1, keepdims=True)
        p = jnp.exp2((s - top) * SCALE).astype(BF16)
        mixed = jnp.dot(p, v, preferred_element_type=F32)
        o = (mixed / mixed[:, HEAD : HEAD + 1]).astype(BF16)
        O[tc] = o.reshape(2, 128, 128)

    slot = lanes(x, yl, core)

    def away(tc, i, other):
        return pltpu.make_async_remote_copy(
            src_ref=O.at[tc, other], dst_ref=OA.at[:, slot],
            send_sem=asend.at[i * 2 + other], recv_sem=arecv.at[i * 2 + core],
            device_id=(r, tc * 2 + other), device_id_type=MESH,
        )

    def block(i, carry):
        tc = lax.rem(chip + i, 8)
        attend(tc)
        away(tc, i, 0).start()
        away(tc, i, 1).start()
        return carry

    lax.fori_loop(1, 2, block, 0)
    pz_pf.wait_recv()
    pz_mf.wait_recv()
    p_xown = WP.at[:, :, :, wide(x)]
    px_p = push(p_xown, xp)
    px_m = push(p_xown, xm)
    lax.fori_loop(2, 6, block, 0)
    f1z_p.wait_recv()
    f1z_pf = push(F1.at[plus(z, 3), 0], zp)
    f1z_m.wait_recv()
    f1z_mf = push(F1.at[plus(z, 1), 1], zm)
    f2y_p.wait_recv()
    yb, yf = plus(y, 3), plus(y, 1)
    f2y_pf = push(F2.at[pl.ds(0, 2), yb // 2, :, cols(lax.rem(yb, 2))], yp)
    f2y_m.wait_recv()
    f2y_mf = push(F2.at[pl.ds(2, 2), yf // 2, :, cols(lax.rem(yf, 2))], ym)
    lax.fori_loop(6, 8, block, 0)
    px_p.wait_recv()
    px_pf = push(WP.at[pl.ds(0, 2), :, :, wide(left)], xp)
    px_m.wait_recv()
    px_mf = push(WP.at[pl.ds(2, 2), :, :, wide(right)], xm)
    attend(chip)
    home = pltpu.make_async_remote_copy(
        src_ref=O.at[chip, 1 - core], dst_ref=OA.at[:, slot],
        send_sem=asend.at[0], recv_sem=arecv.at[core],
        device_id=dd, device_id_type=MESH,
    )
    home.start()
    OA[:, slot] = O[chip, core]

    px_pf.wait_recv()
    px_mf.wait_recv()
    p_half_own = WP.at[:, :, :, pl.ds(pl.multiple_of(core * 1024, 1024), 1024)]
    p_d = push(p_half_own, dd)

    def arrived(i, other):
        pltpu.make_async_remote_copy(
            src_ref=O.at[0, 0], dst_ref=OA.at[:, slot],
            send_sem=asend.at[i * 2], recv_sem=arecv.at[i * 2 + other],
            device_id=dd, device_id_type=MESH,
        ).wait_recv()

    arrived(0, 1 - core)

    def arrivals(i, carry):
        arrived(i, 0)
        arrived(i, 1)
        return carry

    lax.fori_loop(1, 8, arrivals, 0)
    p_d.wait_recv()

    summed = lax.dot_general(OA[...], WP[...].reshape(D, 2048), NT, preferred_element_type=F32)
    resid = tok[...].astype(F32) + summed + prm[2:3, :]
    RES[...] = resid
    H[x, core] = norm(resid, prm[3:4, :], prm[4:5, :]).astype(BF16)

    h_own = H.at[x, core]
    h_p = push(h_own, xp)
    h_m = push(h_own, xm)
    h_d = push(h_own, dd)

    for copy in (f1z_pf, f1z_mf, f2y_pf, f2y_mf, b_y):
        copy.wait_recv()

    def mlp(k, where):
        h = H[where].reshape(256, D)
        a = jnp.dot(h, F1[...].reshape(D, 768), preferred_element_type=F32)
        a = a + jnp.concatenate([FB[0, 0:1, :], FB[1, 0:1, :]], axis=1)
        hidden = (0.5 * a * (1.0 + lax.erf(a * 0.7071067811865476))).astype(BF16)
        part = lax.dot_general(hidden, F2[...].reshape(D, 768), NT, preferred_element_type=F32)
        PART[k] = part.reshape(2, 128, D)
        SS[k] = PART[k, 1 - core].astype(BF16)
        return go(SS.at[k], SD.at[k], dd)

    h_d.wait_recv()
    s_own = mlp(0, x)
    h_p.wait_recv()
    h_pf = push(H.at[left, core, pl.ds(0, 64)], xp)
    hl_d = push(H.at[left, core], dd)
    h_m.wait_recv()
    h_mf = push(H.at[right, core, pl.ds(64, 64)], xm)
    hr_d = push(H.at[right, core], dd)
    hl_d.wait_recv()
    s_l = mlp(1, left)
    hr_d.wait_recv()
    s_r = mlp(2, right)
    h_pf.wait_recv()
    h_mf.wait_recv()
    hf_d = push(H.at[far, core], dd)

    top, low = slice(0, 64), slice(64, 128)
    s_l.wait_recv()
    total = PART[1, core] + SD[1].astype(F32)
    MS[top] = total[top].astype(BF16)
    KEEP[1] = total[low]
    m_a = go(MS.at[top], RR.at[top], xm)
    s_r.wait_recv()
    total = PART[2, core] + SD[2].astype(F32)
    PS[low] = total[low].astype(BF16)
    KEEP[0] = total[top]
    p_b = go(PS.at[low], RL.at[low], xp)

    hf_d.wait_recv()
    s_f = mlp(3, far)
    s_f.wait_recv()
    D2S[...] = (PART[3, core] + SD[3].astype(F32)).astype(BF16)
    d_a = go(D2S.at[top], RA, xp)
    d_b = go(D2S.at[low], RB, xm)
    s_own.wait_recv()
    RES[...] = RES[...] + (PART[0, core] + SD[0].astype(F32)) + prm[5:6, :]

    d_a.wait_recv()
    PS[top] = (KEEP[0] + RA[...].astype(F32)).astype(BF16)
    p_a = go(PS.at[top], RL.at[top], xp)
    d_b.wait_recv()
    MS[low] = (KEEP[1] + RB[...].astype(F32)).astype(BF16)
    m_b = go(MS.at[low], RR.at[low], xm)

    for copy in (m_a, p_b, p_a, m_b):
        copy.wait_recv()
    out[...] = (RES[...] + RL[...].astype(F32) + RR[...].astype(F32)).astype(BF16)

    for copy in started:
        copy.wait_send()

    def sent(i, carry):
        away(0, i, 0).wait_send()
        away(0, i, 1).wait_send()
        return carry

    lax.fori_loop(1, 8, sent, 0)
    home.wait_send()
    assert len(started) <= COPIES


def local(
    tokens_in, ln1_gain, ln1_bias, qkv_weight, qkv_bias, proj_weight, proj_bias,
    ln2_gain, ln2_bias, fc1_weight, fc1_bias, fc2_weight, fc2_bias,
):
    wq = jnp.pad(qkv_weight.reshape(176, 3, HEAD), ((0, 0), (0, 0), (0, 128 - HEAD)))
    wq = wq.reshape(176, 384)
    wp = jnp.pad(proj_weight.T, ((0, 0), (0, 128 - HEAD)))
    bq = jnp.pad(qkv_bias.reshape(3, HEAD).astype(F32), ((0, 0), (0, 128 - HEAD)))
    bq = bq.at[2, HEAD].set(1.0).reshape(384)
    last = jnp.concatenate([bq, fc1_bias.astype(F32), jnp.zeros((D - 768,), F32)])
    rows = [ln1_gain, ln1_bias, proj_bias, ln2_gain, ln2_bias, fc2_bias]
    prm = jnp.stack([v.astype(F32) for v in rows] + [last, last])

    vmem = pl.BlockSpec(memory_space=pltpu.VMEM)
    hbm = pl.BlockSpec(memory_space=pl.ANY)
    dma = pltpu.SemaphoreType.DMA
    scratch = [
        pltpu.VMEM((8, 2, 128, D), BF16),
        pltpu.VMEM((4, 2, 176, 384), BF16),
        pltpu.VMEM((4, 2, 176, 2048), BF16),
        pltpu.VMEM((4, 2, 176, 768), BF16),
        pltpu.VMEM((4, 2, 176, 768), BF16),
        pltpu.VMEM((2, 8, 384), F32),
        pltpu.VMEM((8, 256, 384), BF16),
        pltpu.VMEM((8, 2, 128, 128), BF16),
        pltpu.VMEM((128, 2048), BF16),
        pltpu.VMEM((128, D), F32),
        pltpu.VMEM((4, 2, 128, D), BF16),
        pltpu.VMEM((4, 2, 128, D), F32),
        pltpu.VMEM((4, 128, D), BF16),
        pltpu.VMEM((4, 128, D), BF16),
        pltpu.VMEM((2, 64, D), F32),
        pltpu.VMEM((128, D), BF16),
        pltpu.VMEM((128, D), BF16),
        pltpu.VMEM((128, D), BF16),
        pltpu.VMEM((64, D), BF16),
        pltpu.VMEM((64, D), BF16),
        pltpu.VMEM((128, D), BF16),
        pltpu.VMEM((128, D), BF16),
        dma((COPIES,)), dma((COPIES,)), dma((16,)), dma((16,)), dma((4,)),
    ]
    return pl.pallas_call(
        kernel,
        out_shape=jax.ShapeDtypeStruct((128, D), BF16),
        in_specs=[vmem, vmem, hbm, hbm, hbm, hbm],
        out_specs=vmem,
        scratch_shapes=scratch,
        compiler_params=pltpu.CompilerParams(
            collective_id=0, has_side_effects=True, vmem_limit_bytes=62 * 1024 * 1024
        ),
    )(tokens_in, prm, wq, wp, fc1_weight, fc2_weight)


def solution(mesh):
    in_specs = (
        P(("row", "col"), None), P(), P(), P("row", "col"), P("col"), P("col", "row"), P(),
        P(), P(), P("row", "col"), P("col"), P("row", "col"), P(),
    )
    return jax.shard_map(
        local, mesh=mesh, in_specs=in_specs, out_specs=P(("row", "col"), None), check_vma=False
    )
```

time: 275 us -> 128 us (0.47)
  waiting for transfers between devices: 145 us -> 0 us
  Pallas kernels: 0 us -> 116 us
  blocking collectives: 48.6 us -> 0 us
  matrix products: 32.7 us -> 0 us
  between operations: 13.4 us -> 0.08 us
  other arithmetic: 13.1 us -> 0.02 us
  starting transfers between devices: 13 us -> 0 us
    pallas_call x0 -> x1, Pallas kernels: none -> 116 us  [local(): pl.pallas_call(kernel, out_shape=jax.ShapeDtypeStruct((128, D), BF16), in...]
    reduce_scatter x1 -> x0, waiting for transfers between devices: 68.7 us -> none  [local(): lax.psum_scatter(project_back(hidden, fc2_full).astype(jnp.bfloat16), 'co...]
    all_to_all x3 -> x0, waiting for transfers between devices: 52.4 us -> none  [the longest x2 52.4 us: copy_for_each(): lax.all_to_all(jnp.broadcast_to(value[None], (size, *value.shape)), axis,...]
    all_to_all x2 -> x0, blocking collectives: 48.6 us -> none  [copy_for_each(): lax.all_to_all(jnp.broadcast_to(value[None], (size, *value.shape)), axis,...]
    dot_general x11 -> x0, matrix products: 32.7 us -> none  [the longest x1 16.4 us: project_back(): lax.dot_general(left, right, (((1,), (1,)), ((), ())), preferred_element_...]
    all_gather x3 -> x0, waiting for transfers between devices: 23.4 us -> none  [the longest x1 20.3 us: local(): proj_whole = lax.all_gather(proj_full, 'col', axis=0, tiled=True)]
    all_to_all x3 -> x0, starting transfers between devices: 12.7 us -> none  [the longest x2 7.15 us: copy_for_each(): lax.all_to_all(jnp.broadcast_to(value[None], (size, *value.shape)), axis,...]
    reduce_sum x9 -> x0, other arithmetic: 6.84 us -> none  [the longest x4 3.29 us: one_block(): probs = (expo / jnp.sum(expo, axis=-1, keepdims=True)).astype(jnp.bfloat16)]
  transfers between devices with their start and end apart: 7 -> 0, of which waited for: 5 -> 0; matrix products, arithmetic and copies ran while one was open for 8% -> 0% of each run, Pallas kernels for 0% -> 0%
where the time goes in v1:
time: 128 us; the launch traced here: 126 us
  Pallas kernels  116 us (91%)
  local copies, waits for them, and re-layouts  9.84 us (8%)
    pallas_call x1, Pallas kernels, local(): pl.pallas_call(kernel, out_shape=jax.ShapeDtypeStruct((128, D), BF16), in...  116 us
    unnamed x21, local copies, waits for them, and re-layouts  6.8 us

profile of v1, /device:TPU:1, one launch (start us, length us, event | category | flops | bytes accessed | tf_op | source)
XLA Modules:
  0.0 126.4 jit_solution(13668353129688460901)
XLA Ops:
  0.0 0.8 convert_element_type.11
  0.8 0.1 scatter.4
  0.9 0.0 copy-start.8
  0.9 0.7 copy-done.8
  1.6 0.0 copy-start.2
  1.6 0.7 copy-done.2
  2.3 0.0 copy-start.3
  2.3 0.7 copy-done.3
  3.0 0.0 copy-start.4
  3.0 0.7 copy-done.4
  3.7 0.0 copy-start.5
  3.7 0.7 copy-done.5
  4.3 0.0 copy-start.6
  4.3 0.7 copy-done.6
  5.0 0.0 copy-start.7
  5.0 0.7 copy-done.7
  5.7 0.0 copy-start.1
  5.7 0.0 copy-start
  5.7 0.7 stack.56.prm
  6.4 0.1 copy-done.1
  6.5 0.1 copy.17
  6.6 0.6 pad.22.wp
  7.3 0.0 copy-done
  7.3 0.1 copy.15
  7.4 0.8 copy.18.wq
  8.2 116.4 %shard_map.127 = bf16[128,1408]{1,0:T(8,128)(2,1)} custom-call(bf16[128,1408]{1,0:T(8,128)(2,1)} %tok.1, f32[8,1408]{1,0:T(8,128)} %stack.56.prm, bf16[176,384]{1,0:T(8,128)(2,1)} %copy.18.wq, bf16[176,128]{1,0:T(8,128)(2,1)} %pad.22.wp, bf16[176,384]{1,0:T(8,128)(2,1)} %f1.1, bf16[176,384]{1,0:T(8,128)(2,1)} %f2.1), custom_call_target="tpu_custom_call" | custom-call | tf_op jit(solution)/shard_map/pallas_call | solution.py:449
  124.6 1.7 %copy.21 = bf16[128,1408]{1,0:T(8,128)(2,1)} copy(bf16[128,1408]{1,0:T(8,128)(2,1)} %shard_map.127) | data formatting | bytes 720896
  (12 shorter events, 0.1 us)
Async XLA Ops:
  0.9 0.7 copy-start.8
  1.6 0.7 copy-start.2
  2.3 0.7 copy-start.3
  3.0 0.7 copy-start.4
  3.7 0.7 copy-start.5
  4.3 0.7 copy-start.6
  5.0 0.7 copy-start.7
  5.7 0.8 copy-start.1
  5.7 1.5 %copy-start = (bf16[176,264]{1,0:T(8,128)(2,1)S(1)}, bf16[176,264]{1,0:T(8,128)(2,1)}, u32[]{:S(2)}) copy-start(bf16[176,264]{1,0:T(8,128)(2,1)} %param.18) | copy-start | bytes 278788
